TPU v7x, 512 devices: a whole 4x8x8 slice. The times are simulated.
512 devices in a mesh: dp: 32 (over y_lo, z), owner: 16 (over x, y_hi, core).
Axes of the slice: x: 4, y: 8 (y_hi: 2, y_lo: 4; y = y_hi * 4 + y_lo), z: 8, core: 2. Of those that a mesh axis runs over, the one named last changes fastest.
Arguments:
- gradients: bfloat16 [32, 16, 512, 512], P('dp', 'owner'), may hold values from -600 to 600
- block_layer: int32 [16], P('owner'), may hold values from 0 to 3
Outputs:
- update: bfloat16 [16, 512, 512], P('owner', 'dp')
All inputs are finite; a program needn't handle non-finite values.
Results may differ from a plain program's by a relative error of at most 0.0062.
Values may be sent and summed in bfloat16 or wider, within the bound.
No kernel may reach another device: no remote copies, remote signals or barrier semaphores. Data moves between devices by JAX's collectives and lax.ppermute only.
A program may use at most 64 MiB of HBM per device.

v0:
```python
import jax
import jax.numpy as jnp
from jax import lax
from jax.sharding import Mesh
from jax.sharding import PartitionSpec as P

LAYERS = 4
ITERS = 3
DP = ("dp_0", "dp_1")
DP_OWNER = ("dp_0", "dp_1", "owner_0", "owner_1", "owner_2")
OWNER = ("owner_0", "owner_1", "owner_2")


def from_partner(x, axis, distance):
    return lax.ppermute(x, axis, [(i, i ^ 1 << distance) for i in range(lax.axis_size(axis))])


def cut_along(x, dim, size):
    lengths = x.shape
    parts = x.reshape(*lengths[:dim], size, lengths[dim] // size, *lengths[dim + 1 :])
    return jnp.moveaxis(parts, dim, 0)


def summed_on_arrival(x, axis, dim):
    parts = cut_along(x, dim, lax.axis_size(axis))
    arrived = lax.all_to_all(parts, axis, split_axis=0, concat_axis=0, tiled=True)
    return arrived.sum(axis=0)


def sent_to_all(x, axis):
    size = lax.axis_size(axis)
    return lax.all_to_all(jnp.broadcast_to(x[None], (size, *x.shape)), axis, 0, 0, tiled=True)


def laid_out(parts, dim):
    lengths = list(parts.shape[1:])
    lengths[dim] *= parts.shape[0]
    return jnp.moveaxis(parts, 0, dim).reshape(lengths)


def gathered_copies(x, axis, dim):
    parts = sent_to_all(x, axis)
    return laid_out(parts, dim)


def by_axis(x, axes):
    for axis in axes:
        x = lax.psum(x, axis)
    return x


def own_whole(partial_rows, position, members):
    gathered = partial_rows
    for bit_number in range(members.bit_length() - 1):
        partner = from_partner(gathered, DP, bit_number)
        upper_half = position // (1 << bit_number) % 2 == 1
        gathered = jnp.where(
            upper_half,
            jnp.concatenate([partner, gathered], axis=0),
            jnp.concatenate([gathered, partner], axis=0),
        )
    return gathered


def keep_whole(partial_rows):
    return partial_rows


def root_slab(stat_rows, eye_rows, assemble):
    size_b = stat_rows.shape[1]
    identity = jnp.eye(size_b, dtype=jnp.float32)
    statistic = assemble(stat_rows)
    ridge_term = 0.01 * jnp.trace(statistic) / size_b + 1e-06
    shifted_whole = statistic + ridge_term * identity
    scaling = jnp.sqrt(jnp.sum(shifted_whole * shifted_whole))
    current_whole = shifted_whole / scaling
    current_rows = (stat_rows + ridge_term * eye_rows) / scaling
    inverse_rows = eye_rows
    for step_number in range(ITERS):
        factor_whole = (5.0 * identity - current_whole) / 4.0
        factor_rows = (5.0 * eye_rows - current_rows) / 4.0
        if step_number == 0:
            inverse_rows = scaling ** (-0.25) * factor_rows
        else:
            inverse_rows = jnp.dot(inverse_rows, factor_whole, precision=lax.Precision.HIGHEST)
        if step_number + 1 < ITERS:
            square_rows = jnp.dot(factor_rows, factor_whole, precision=lax.Precision.HIGHEST)
            square_whole = assemble(square_rows)
            fourth_rows = jnp.dot(square_rows, square_whole, precision=lax.Precision.HIGHEST)
            current_rows = jnp.dot(fourth_rows, current_whole, precision=lax.Precision.HIGHEST)
            current_whole = assemble(current_rows)
    return inverse_rows


def per_device(gradients, block_layer):
    gradient = gradients[0, 0]
    size_b = gradient.shape[0]
    dp_count = lax.axis_size(DP)
    members = dp_count // 2
    height = size_b // members
    position = lax.axis_index(DP)
    offset = position % members * height
    left_gram = lax.dot_general(
        gradient, gradient, (((1,), (1,)), ((), ())), preferred_element_type=jnp.float32
    )
    right_gram = lax.dot_general(
        gradient, gradient, (((0,), (0,)), ((), ())), preferred_element_type=jnp.float32
    )
    stacked = jnp.concatenate([left_gram, right_gram], axis=0)
    half_rows = summed_on_arrival(stacked, DP, 0)
    statistic = own_whole(half_rows, position, members)
    inverse_whole = root_slab(statistic, jnp.eye(size_b, dtype=jnp.float32), keep_whole)
    inverse_rows = lax.dynamic_slice_in_dim(inverse_whole, offset, height, 0)
    both_roots = gathered_copies(inverse_rows.astype(jnp.bfloat16), DP, 0)
    left_root = both_roots[:size_b]
    right_root = both_roots[size_b:]
    out_height = size_b // dp_count
    right_wide = right_root.astype(jnp.float32)
    left_part = lax.slice_in_dim(left_root, 0, out_height * lax.axis_size(DP), axis=0)
    middle = jnp.dot(left_part, gradient, preferred_element_type=jnp.float32)
    summed = summed_on_arrival(jnp.dot(middle, right_wide, precision=lax.Precision.HIGHEST), DP, 0)
    precond = summed / dp_count
    layer_id = block_layer[0]
    selector = (jnp.arange(LAYERS, dtype=jnp.int32) == layer_id).astype(jnp.float32)
    energy = jnp.sum(precond * precond)
    totals_sq, counts = (
        by_axis(selector * energy, DP_OWNER),
        by_axis(selector * float(precond.size), DP_OWNER),
    )
    mean_square = jnp.sum(selector * totals_sq) / jnp.sum(selector * counts)
    update = (precond * lax.rsqrt(mean_square + 1e-06)).astype(jnp.bfloat16)
    return update[None]


def solution(mesh):
    finer = Mesh(
        mesh.devices.reshape(4, 8, 4, 2, 2), ("dp_0", "dp_1", "owner_0", "owner_1", "owner_2")
    )
    in_specs = (P(DP, OWNER, None, None), P(OWNER))
    out_specs = P(OWNER, DP, None)
    return jax.shard_map(
        per_device, mesh=finer, in_specs=in_specs, out_specs=out_specs, check_vma=False
    )
```

profile of v0, /device:TPU:1, one launch (start us, length us, event | category | flops | bytes accessed | tf_op | source)
XLA Modules:
  0.0 257.0 jit_solution(7543262102058566053)
XLA Ops:
  0.0 0.0 copy-start
  0.0 1.0 copy-done
  1.0 0.5 fusion.12
  1.5 0.5 fusion.14
  2.0 0.2 pad_maximum_fusion
  2.2 62.1 %all_to_all.15 = f32[32,32,512]{2,1,0:T(8,128)S(1)} all-to-all(f32[32,32,512]{2,1,0:T(8,128)S(1)} %bitcast.32), channel_id=1, replica_groups=mesh['dp_0'=4,'dp_1'=8,'owner_0'=4,'owner_1'=2,'owner_2'=2] {'dp_0','dp_1'}, dimensions={0} | all-to-all | bytes 4194304 | tf_op jit(solution)/shard_map/all_to_all | solution.py:26
  64.3 0.1 reduce_sum.64
  64.4 4.5 %collective-permute-start = (f32[32,512]{1,0:T(8,128)S(1)}, f32[32,512]{1,0:T(8,128)S(1)}, u32[]{:S(2)}, u32[]{:S(2)}) collective-permute-start(f32[32,512]{1,0:T(8,128)S(1)} %reduce_sum.64), channel_id=1, source_target_pairs={{0,16},{16,0},{32,48},{48,32},{64,80},{80,64},{96,112},{112,96},{1... | collective-permute-start | bytes 196616 | tf_op jit(solution)/shard_map/ppermute | solution.py:15
  68.9 1.6 collective-permute-done
  70.6 4.3 %collective-permute-start.1 = (f32[64,512]{1,0:T(8,128)S(1)}, f32[64,512]{1,0:T(8,128)S(1)}, u32[]{:S(2)}, u32[]{:S(2)}) collective-permute-start(f32[64,512]{1,0:T(8,128)S(1)} %maximum_select_fusion.3), channel_id=1, source_target_pairs={{0,32},{16,48},{32,0},{48,16},{64,96},{80,112},{96,64},{112,80},{1... | collective-permute-start | bytes 393224 | tf_op jit(solution)/shard_map/ppermute | solution.py:15
  74.9 3.7 %collective-permute-done.1 = f32[64,512]{1,0:T(8,128)S(1)} collective-permute-done((f32[64,512]{1,0:T(8,128)S(1)}, f32[64,512]{1,0:T(8,128)S(1)}, u32[]{:S(2)}, u32[]{:S(2)}) %collective-permute-start.1) | collective-permute-done | bytes 131104 | tf_op jit(solution)/shard_map/ppermute | solution.py:15
  78.7 5.4 %collective-permute-start.2 = (f32[128,512]{1,0:T(8,128)S(1)}, f32[128,512]{1,0:T(8,128)S(1)}, u32[]{:S(2)}, u32[]{:S(2)}) collective-permute-start(f32[128,512]{1,0:T(8,128)S(1)} %maximum_select_fusion.2), channel_id=1, source_target_pairs={{0,64},{16,80},{32,96},{48,112},{64,0},{80,16},{96,32},{112,48},{1... | collective-permute-start | bytes 786440 | tf_op jit(solution)/shard_map/ppermute | solution.py:15
  84.1 12.8 %collective-permute-done.2 = f32[128,512]{1,0:T(8,128)S(1)} collective-permute-done((f32[128,512]{1,0:T(8,128)S(1)}, f32[128,512]{1,0:T(8,128)S(1)}, u32[]{:S(2)}, u32[]{:S(2)}) %collective-permute-start.2) | collective-permute-done | bytes 262176 | tf_op jit(solution)/shard_map/ppermute | solution.py:15
  96.9 1.9 collective-permute-start.3
  98.9 11.8 %collective-permute-done.3 = f32[256,512]{1,0:T(8,128)S(1)} collective-permute-done((f32[256,512]{1,0:T(8,128)S(1)}, f32[256,512]{1,0:T(8,128)S(1)}, u32[]{:S(2)}, u32[]{:S(2)}) %collective-permute-start.3) | collective-permute-done | bytes 524320 | tf_op jit(solution)/shard_map/ppermute | solution.py:15
  110.7 0.0 copy-start.1
  110.7 0.7 select_reduce_fusion
  112.0 0.9 multiply_reduce_fusion
  113.6 2.1 fusion.2
  115.7 2.8 %fusion.43 = f32[512,512]{1,0:T(8,128)} fusion(f32[512,512]{1,0:T(8,128)S(1)} %fusion.2), kind=kOutput, calls=%fused_computation.56 | convolution fusion | flops 1610612736 | bytes 2097152 | tf_op jit(solution)/shard_map/dot_general | solution.py:89
  118.6 0.0 copy-done.1
  118.6 3.2 %fusion.39 = f32[512,512]{1,0:T(8,128)S(1)} fusion(f32[512,512]{1,0:T(8,128)} %fusion.43, f32[]{:T(128)S(6)} %sqrt.3, f32[]{:T(128)S(6)} %add.61, f32[256,512]{1,0:T(8,128)S(1)} %collective-permute-done.3, f32[256,512]{1,0:T(8,128)S(1)} %maximum_select_fusion.1, pred[]{:T(512)S(6)} %eq.39), kind=kOutput, calls=%fused_computation.54 | convolution fusion | flops 1612447744 | bytes 3145737 | tf_op jit(solution)/shard_map/dot_general | solution.py:90
  121.8 1.9 fusion.7
  123.7 1.8 fusion.44
  125.5 1.9 fusion
  127.4 3.3 %fusion.4 = f32[512,512]{1,0:T(8,128)S(1)} fusion(f32[512,512]{1,0:T(8,128)S(1)} %fusion.39, f32[]{:T(128)S(6)} %mul.75, f32[]{:T(128)S(6)} %sqrt.3, f32[]{:T(128)S(6)} %add.61, f32[256,512]{1,0:T(8,128)} %copy-done.1, f32[256,512]{1,0:T(8,128)S(1)} %maximum_select_fusion.1, pred[]{:T(512)S(6)} %eq.39), kind=kOutput, calls=%fused_computation.9 | convolution fusion | flops 1614282752 | bytes 3145741 | tf_op jit(solution)/shard_map/dot_general | solution.py:85
  130.7 2.0 fusion.45
  132.7 0.1 broadcast_in_dim.4
  132.9 32.6 %all_to_all.16 = bf16[32,32,512]{2,1,0:T(8,128)(2,1)S(1)} all-to-all(bf16[32,32,512]{2,1,0:T(8,128)(2,1)S(1)} %broadcast_in_dim.4), channel_id=1, replica_groups=mesh['dp_0'=4,'dp_1'=8,'owner_0'=4,'owner_1'=2,'owner_2'=2] {'dp_0','dp_1'}, dimensions={0} | all-to-all | bytes 2097152 | tf_op jit(solution)/shard_map/all_to_all | solution.py:32
  165.4 0.1 fusion.42
  165.6 0.4 fusion.10
  166.0 2.0 fusion.46
  168.0 8.0 %all-to-all-start.2 = ((f32[32,16,512]{2,1,0:T(8,128)}), f32[32,16,512]{2,1,0:T(8,128)S(1)}, u32[]{:S(2)}, u32[]{:S(2)}) async-start(f32[32,16,512]{2,1,0:T(8,128)} %fusion.46), calls=%async_computation.2 | async-start | bytes 2097152 | tf_op jit(solution)/shard_map/all_to_all | solution.py:26
  176.6 25.2 %all-to-all-done.2 = f32[32,16,512]{2,1,0:T(8,128)S(1)} async-done(((f32[32,16,512]{2,1,0:T(8,128)}), f32[32,16,512]{2,1,0:T(8,128)S(1)}, u32[]{:S(2)}, u32[]{:S(2)}) %all-to-all-start.2) | async-done | bytes 1048608 | tf_op jit(solution)/shard_map/all_to_all | solution.py:26
  201.8 0.1 reduce_sum.67
  201.8 0.6 multiply_reduce_fusion.1
  202.5 0.6 fusion.28
  203.1 10.3 %all-reduce.2 = (f32[4]{0:T(128)S(1)}, f32[4]{0:T(128)S(1)}) all-reduce(f32[4]{0:T(128)S(1)} %fusion.28, f32[4]{0:T(128)S(1)} %fusion.27), channel_id=1, replica_groups=mesh['dp_0'=4,'dp_1'=8,'owner_0'=4,'owner_1'=2,'owner_2'=2] {'dp_0'}, use_global_device_ids=true, to_apply=%region_5.6 | all-reduce | flops 8 | bytes 64 | tf_op jit(solution)/shard_map/psum | solution.py:48
  213.4 13.0 %all-reduce = (f32[4]{0:T(128)S(1)}, f32[4]{0:T(128)S(1)}) all-reduce(f32[4]{0:T(128)S(1)} %get-tuple-element.9, f32[4]{0:T(128)S(1)} %get-tuple-element.10), channel_id=1, replica_groups=mesh['dp_0'=4,'dp_1'=8,'owner_0'=4,'owner_1'=2,'owner_2'=2] {'dp_1'}, use_global_device_ids=true, to_apply=%region_6.7 | all-reduce | flops 8 | bytes 64 | tf_op jit(solution)/shard_map/psum | solution.py:48
  226.4 8.9 %all-reduce.1 = (f32[4]{0:T(128)S(1)}, f32[4]{0:T(128)S(1)}) all-reduce(f32[4]{0:T(128)S(1)} %get-tuple-element.5, f32[4]{0:T(128)S(1)} %get-tuple-element.6), channel_id=1, replica_groups=mesh['dp_0'=4,'dp_1'=8,'owner_0'=4,'owner_1'=2,'owner_2'=2] {'owner_0'}, use_global_device_ids=true, to_apply=%region_7.8 | all-reduce | flops 8 | bytes 64 | tf_op jit(solution)/shard_map/psum | solution.py:48
  235.3 7.7 %all-reduce.4 = (f32[4]{0:T(128)S(1)}, f32[4]{0:T(128)S(1)}) all-reduce(f32[4]{0:T(128)S(1)} %get-tuple-element.7, f32[4]{0:T(128)S(1)} %get-tuple-element.8), channel_id=1, replica_groups=mesh['dp_0'=4,'dp_1'=8,'owner_0'=4,'owner_1'=2,'owner_2'=2] {'owner_1'}, use_global_device_ids=true, to_apply=%region_8.9 | all-reduce | flops 8 | bytes 64 | tf_op jit(solution)/shard_map/psum | solution.py:48
  243.0 11.3 %all-reduce.3 = (f32[4]{0:T(128)S(1)}, f32[4]{0:T(128)S(1)}) all-reduce(f32[4]{0:T(128)S(1)} %get-tuple-element.13, f32[4]{0:T(128)S(1)} %get-tuple-element.14), channel_id=1, replica_groups=mesh['dp_0'=4,'dp_1'=8,'owner_0'=4,'owner_1'=2,'owner_2'=2] {'owner_2'}, use_global_device_ids=true, to_apply=%region_9.10 | all-reduce | flops 8 | bytes 64 | tf_op jit(solution)/shard_map/psum | solution.py:48
  254.3 0.7 select_reduce_fusion.1
  256.4 0.6 fusion.26
  (5 shorter events, 0.1 us)
Async XLA Ops:
  0.0 1.0 copy-start
  64.4 6.1 %collective-permute-start = (f32[32,512]{1,0:T(8,128)S(1)}, f32[32,512]{1,0:T(8,128)S(1)}, u32[]{:S(2)}, u32[]{:S(2)}) collective-permute-start(f32[32,512]{1,0:T(8,128)S(1)} %reduce_sum.64), channel_id=1, source_target_pairs={{0,16},{16,0},{32,48},{48,32},{64,80},{80,64},{96,112},{112,96},{1... | collective-permute-start | bytes 196616 | tf_op jit(solution)/shard_map/ppermute | solution.py:15
  70.6 8.1 %collective-permute-start.1 = (f32[64,512]{1,0:T(8,128)S(1)}, f32[64,512]{1,0:T(8,128)S(1)}, u32[]{:S(2)}, u32[]{:S(2)}) collective-permute-start(f32[64,512]{1,0:T(8,128)S(1)} %maximum_select_fusion.3), channel_id=1, source_target_pairs={{0,32},{16,48},{32,0},{48,16},{64,96},{80,112},{96,64},{112,80},{1... | collective-permute-start | bytes 393224 | tf_op jit(solution)/shard_map/ppermute | solution.py:15
  78.7 18.2 %collective-permute-start.2 = (f32[128,512]{1,0:T(8,128)S(1)}, f32[128,512]{1,0:T(8,128)S(1)}, u32[]{:S(2)}, u32[]{:S(2)}) collective-permute-start(f32[128,512]{1,0:T(8,128)S(1)} %maximum_select_fusion.2), channel_id=1, source_target_pairs={{0,64},{16,80},{32,96},{48,112},{64,0},{80,16},{96,32},{112,48},{1... | collective-permute-start | bytes 786440 | tf_op jit(solution)/shard_map/ppermute | solution.py:15
  96.9 13.8 %collective-permute-start.3 = (f32[256,512]{1,0:T(8,128)S(1)}, f32[256,512]{1,0:T(8,128)S(1)}, u32[]{:S(2)}, u32[]{:S(2)}) collective-permute-start(f32[256,512]{1,0:T(8,128)S(1)} %maximum_select_fusion.1), channel_id=1, source_target_pairs={{0,128},{16,144},{32,160},{48,176},{64,192},{80,208},{96,224},{112... | collective-permute-start | bytes 1572872 | tf_op jit(solution)/shard_map/ppermute | solution.py:15
  110.7 7.9 %copy-start.1 = (f32[256,512]{1,0:T(8,128)}, f32[256,512]{1,0:T(8,128)S(1)}, u32[]{:S(2)}) copy-start(f32[256,512]{1,0:T(8,128)S(1)} %collective-permute-done.3) | copy-start | bytes 1572868
  168.0 33.8 %all-to-all-start.2 = ((f32[32,16,512]{2,1,0:T(8,128)}), f32[32,16,512]{2,1,0:T(8,128)S(1)}, u32[]{:S(2)}, u32[]{:S(2)}) async-start(f32[32,16,512]{2,1,0:T(8,128)} %fusion.46), calls=%async_computation.2 | async-start | bytes 2097152 | tf_op jit(solution)/shard_map/all_to_all | solution.py:26
where the time goes:
time: 258 us; the launch traced here: 257 us
  blocking collectives  146 us (57%)
  waiting for transfers between devices  55.1 us (21%)
  starting transfers between devices  24.1 us (9%)
  matrix products  22.3 us (9%)
  other arithmetic  4.59 us (2%)
  between operations  3.79 us (1%)
    all_to_all x1, blocking collectives, summed_on_arrival(): lax.all_to_all(parts, axis, split_axis=0, concat_axis=0, tiled=True)  62.1 us
    psum x5, blocking collectives, by_axis(): x = lax.psum(x, axis)  51.1 us
    all_to_all x1, blocking collectives, sent_to_all(): lax.all_to_all(jnp.broadcast_to(x[None], (size, *x.shape)), axis, 0, 0, t...  32.6 us
    ppermute x4, waiting for transfers between devices, from_partner(): lax.ppermute(x, axis, [(i, i ^ 1 << distance) for i in range(lax.axis_siz...  29.9 us
    all_to_all x1, waiting for transfers between devices, summed_on_arrival(): lax.all_to_all(parts, axis, split_axis=0, concat_axis=0, tiled=True)  25.2 us
    ppermute x4, starting transfers between devices, from_partner(): lax.ppermute(x, axis, [(i, i ^ 1 << distance) for i in range(lax.axis_siz...  16.1 us
    all_to_all x1, starting transfers between devices, summed_on_arrival(): lax.all_to_all(parts, axis, split_axis=0, concat_axis=0, tiled=True)  7.95 us
    dot_general x2, matrix products, root_slab(): jnp.dot(inverse_rows, factor_whole, precision=lax.Precision.HIGHEST)  5.3 us
  transfers between devices with their start and end apart: 5, of which 5 were waited for; matrix products, arithmetic and copies ran while one was open for 0% of the time, Pallas kernels for 0%

commit v1 on v0

--- a/solution.py
+++ b/solution.py
@@ -45,7 +45,7 @@
 
 def by_axis(x, axes):
     for axis in axes:
-        x = lax.psum(x, axis)
+        x = jnp.sum(lax.all_gather(x, axis), axis=0)
     return x
 
 

time: 258 us -> 274 us (1.062)
  blocking collectives: 146 us -> 114 us
  waiting for transfers between devices: 55.1 us -> 80.2 us
  starting transfers between devices: 24.1 us -> 35.1 us
  local copies, waits for them, and re-layouts: 1.27 us -> 8.85 us
    all_to_all x1 -> x0, blocking collectives: 62.1 us -> none  [summed_on_arrival(): lax.all_to_all(parts, axis, split_axis=0, concat_axis=0, tiled=True)]
    psum x5 -> x0, blocking collectives: 51.1 us -> none  [by_axis(): x = lax.psum(x, axis)]
    unnamed x0 -> x4, blocking collectives: none -> 45.4 us
    all_gather x0 -> x2, blocking collectives: none -> 33.5 us  [by_axis(): x = jnp.sum(lax.all_gather(x, axis), axis=0)]
    all_to_all x1 -> x2, waiting for transfers between devices: 25.2 us -> 54.4 us  [summed_on_arrival(): lax.all_to_all(parts, axis, split_axis=0, concat_axis=0, tiled=True)]
    all_to_all x1 -> x2, starting transfers between devices: 7.95 us -> 22.3 us  [summed_on_arrival(): lax.all_to_all(parts, axis, split_axis=0, concat_axis=0, tiled=True)]
    unnamed x4 -> x24, local copies, waits for them, and re-layouts: 1.05 us -> 7.97 us
    ppermute x4, waiting for transfers between devices: 29.9 us -> 25.8 us  [from_partner(): lax.ppermute(x, axis, [(i, i ^ 1 << distance) for i in range(lax.axis_siz...]
  transfers between devices with their start and end apart: 5 -> 6, of which waited for: 5 -> 5; matrix products, arithmetic and copies ran while one was open for 0% -> 2% of each run, Pallas kernels for 0% -> 0%
where the time goes in v1:
time: 274 us; the launch traced here: 273 us
  blocking collectives  114 us (42%)
  waiting for transfers between devices  80.2 us (29%)
  starting transfers between devices  35.1 us (13%)
  matrix products  22.3 us (8%)
  local copies, waits for them, and re-layouts  8.85 us (3%)
  between operations  6.34 us (2%)
  other arithmetic  6.14 us (2%)
    all_to_all x2, waiting for transfers between devices, summed_on_arrival(): lax.all_to_all(parts, axis, split_axis=0, concat_axis=0, tiled=True)  54.4 us
    unnamed x4, blocking collectives  45.4 us
    all_to_all x1, blocking collectives, sent_to_all(): lax.all_to_all(jnp.broadcast_to(x[None], (size, *x.shape)), axis, 0, 0, t...  35.6 us
    all_gather x2, blocking collectives, by_axis(): x = jnp.sum(lax.all_gather(x, axis), axis=0)  33.5 us
    ppermute x4, waiting for transfers between devices, from_partner(): lax.ppermute(x, axis, [(i, i ^ 1 << distance) for i in range(lax.axis_siz...  25.8 us
    all_to_all x2, starting transfers between devices, summed_on_arrival(): lax.all_to_all(parts, axis, split_axis=0, concat_axis=0, tiled=True)  22.3 us
    ppermute x4, starting transfers between devices, from_partner(): lax.ppermute(x, axis, [(i, i ^ 1 << distance) for i in range(lax.axis_siz...  12.8 us
    unnamed x24, local copies, waits for them, and re-layouts  7.97 us
  transfers between devices with their start and end apart: 6, of which 5 were waited for; matrix products, arithmetic and copies ran while one was open for 2% of the time, Pallas kernels for 0%

profile of v1, /device:TPU:1, one launch (start us, length us, event | category | flops | bytes accessed | tf_op | source)
XLA Modules:
  0.0 273.4 jit_solution(2825666327140643382)
XLA Ops:
  0.0 1.0 copy-done
  1.0 0.5 fusion.12
  1.5 0.5 fusion.14
  2.0 1.5 pad_maximum_fusion
  3.5 14.3 %all-to-all-start = ((f32[32,32,512]{2,1,0:T(8,128)}), f32[32,32,512]{2,1,0:T(8,128)S(1)}, u32[]{:S(2)}, u32[]{:S(2)}) async-start(f32[32,32,512]{2,1,0:T(8,128)} %bitcast.40), calls=%async_computation | async-start | bytes 4194304 | tf_op jit(solution)/shard_map/all_to_all | solution.py:26
  17.8 54.4 %all-to-all-done = f32[32,32,512]{2,1,0:T(8,128)S(1)} async-done(((f32[32,32,512]{2,1,0:T(8,128)}), f32[32,32,512]{2,1,0:T(8,128)S(1)}, u32[]{:S(2)}, u32[]{:S(2)}) %all-to-all-start) | async-done | bytes 2097184 | tf_op jit(solution)/shard_map/all_to_all | solution.py:26
  72.3 2.0 collective-permute-start
  74.4 2.9 %collective-permute-done = f32[32,512]{1,0:T(8,128)S(1)} collective-permute-done((f32[32,512]{1,0:T(8,128)S(1)}, f32[32,512]{1,0:T(8,128)S(1)}, u32[]{:S(2)}, u32[]{:S(2)}) %collective-permute-start) | collective-permute-done | bytes 65568 | tf_op jit(solution)/shard_map/ppermute | solution.py:15
  77.3 2.0 collective-permute-start.1
  79.4 5.8 %collective-permute-done.1 = f32[64,512]{1,0:T(8,128)S(1)} collective-permute-done((f32[64,512]{1,0:T(8,128)S(1)}, f32[64,512]{1,0:T(8,128)S(1)}, u32[]{:S(2)}, u32[]{:S(2)}) %collective-permute-start.1) | collective-permute-done | bytes 131104 | tf_op jit(solution)/shard_map/ppermute | solution.py:15
  85.2 6.1 %collective-permute-start.2 = (f32[128,512]{1,0:T(8,128)S(1)}, f32[128,512]{1,0:T(8,128)S(1)}, u32[]{:S(2)}, u32[]{:S(2)}) collective-permute-start(f32[128,512]{1,0:T(8,128)S(1)} %maximum_select_fusion.2), channel_id=1, source_target_pairs={{0,64},{16,80},{32,96},{48,112},{64,0},{80,16},{96,32},{112,48},{1... | collective-permute-start | bytes 786440 | tf_op jit(solution)/shard_map/ppermute | solution.py:15
  91.3 8.7 %collective-permute-done.2 = f32[128,512]{1,0:T(8,128)S(1)} collective-permute-done((f32[128,512]{1,0:T(8,128)S(1)}, f32[128,512]{1,0:T(8,128)S(1)}, u32[]{:S(2)}, u32[]{:S(2)}) %collective-permute-start.2) | collective-permute-done | bytes 262176 | tf_op jit(solution)/shard_map/ppermute | solution.py:15
  100.1 2.6 collective-permute-start.3
  102.8 8.3 %collective-permute-done.3 = f32[256,512]{1,0:T(8,128)S(1)} collective-permute-done((f32[256,512]{1,0:T(8,128)S(1)}, f32[256,512]{1,0:T(8,128)S(1)}, u32[]{:S(2)}, u32[]{:S(2)}) %collective-permute-start.3) | collective-permute-done | bytes 524320 | tf_op jit(solution)/shard_map/ppermute | solution.py:15
  111.1 0.7 select_reduce_fusion
  112.5 0.9 multiply_reduce_fusion
  114.1 2.1 fusion.2
  116.1 2.8 %fusion.45 = f32[512,512]{1,0:T(8,128)} fusion(f32[512,512]{1,0:T(8,128)S(1)} %fusion.2), kind=kOutput, calls=%fused_computation.59 | convolution fusion | flops 1610612736 | bytes 2097152 | tf_op jit(solution)/shard_map/dot_general | solution.py:89
  119.1 3.2 %fusion.41 = f32[512,512]{1,0:T(8,128)S(1)} fusion(f32[512,512]{1,0:T(8,128)} %fusion.45, f32[]{:T(128)S(6)} %sqrt.3, f32[]{:T(128)S(6)} %add.41, f32[256,512]{1,0:T(8,128)S(1)} %collective-permute-done.3, f32[256,512]{1,0:T(8,128)S(1)} %maximum_select_fusion.1, pred[]{:T(512)S(6)} %eq.54), kind=kOutput, calls=%fused_computation.57 | convolution fusion | flops 1612447744 | bytes 3145737 | tf_op jit(solution)/shard_map/dot_general | solution.py:90
  122.2 1.9 fusion.7
  124.1 1.8 fusion.46
  126.0 1.9 fusion
  127.8 3.3 %fusion.4 = f32[512,512]{1,0:T(8,128)S(1)} fusion(f32[512,512]{1,0:T(8,128)S(1)} %fusion.41, f32[]{:T(128)S(6)} %mul.75, f32[]{:T(128)S(6)} %sqrt.3, f32[]{:T(128)S(6)} %add.41, f32[256,512]{1,0:T(8,128)} %copy-done.1, f32[256,512]{1,0:T(8,128)S(1)} %maximum_select_fusion.1, pred[]{:T(512)S(6)} %eq.54), kind=kOutput, calls=%fused_computation.9 | convolution fusion | flops 1614282752 | bytes 3145741 | tf_op jit(solution)/shard_map/dot_general | solution.py:85
  131.1 2.0 fusion.47
  133.3 35.6 %all_to_all.15 = bf16[32,32,512]{2,1,0:T(8,128)(2,1)S(1)} all-to-all(bf16[32,32,512]{2,1,0:T(8,128)(2,1)S(1)} %broadcast_in_dim.4), channel_id=1, replica_groups=mesh['dp_0'=4,'dp_1'=8,'owner_0'=4,'owner_1'=2,'owner_2'=2] {'dp_0','dp_1'}, dimensions={0} | all-to-all | bytes 2097152 | tf_op jit(solution)/shard_map/all_to_all | solution.py:32
  169.0 0.4 fusion.10
  169.4 2.0 fusion.48
  171.4 8.0 %all-to-all-start.2 = ((f32[32,16,512]{2,1,0:T(8,128)}), f32[32,16,512]{2,1,0:T(8,128)S(1)}, u32[]{:S(2)}, u32[]{:S(2)}) async-start(f32[32,16,512]{2,1,0:T(8,128)} %fusion.48), calls=%async_computation.2 | async-start | bytes 2097152 | tf_op jit(solution)/shard_map/all_to_all | solution.py:26
  180.1 22.2 %all-gather.9 = f32[4,1,4]{2,1,0:T(1,128)S(1)} all-gather(f32[1,1,4]{2,1,0:T(1,128)S(1)} %fusion.28), channel_id=1, replica_groups=mesh['dp_0'=4,'dp_1'=8,'owner_0'=4,'owner_1'=2,'owner_2'=2] {'dp_0'}, dimensions={0}, use_global_device_ids=true | all-gather | bytes 80 | tf_op jit(solution)/shard_map/all_gather | solution.py:48
  202.3 1.3 dynamic-slice
  203.6 1.2 dynamic-slice.1
  206.0 1.3 dynamic-slice.2
  208.0 1.3 dynamic-slice.3
  209.4 0.6 multiply_reduce_fusion.1
  210.0 0.6 fusion.27
  210.7 0.2 dynamic-update-slice.4
  210.9 11.3 %all-gather.8 = f32[4,1,4]{2,1,0:T(1,128)S(1)} all-gather(f32[1,1,4]{2,1,0:T(1,128)S(1)} %fusion.27), channel_id=1, replica_groups=mesh['dp_0'=4,'dp_1'=8,'owner_0'=4,'owner_1'=2,'owner_2'=2] {'dp_0'}, dimensions={0}, use_global_device_ids=true | all-gather | bytes 80 | tf_op jit(solution)/shard_map/all_gather | solution.py:48
  222.2 0.2 dynamic-update-slice
  222.4 13.0 %all-reduce.8 = (f32[32]{0:T(128)S(1)}, f32[32]{0:T(128)S(1)}) all-reduce(f32[32]{0:T(128)S(1)} %dynamic-update-slice, f32[32]{0:T(128)S(1)} %dynamic-update-slice.4), channel_id=2, replica_groups=mesh['dp_0'=4,'dp_1'=8,'owner_0'=4,'owner_1'=2,'owner_2'=2] {'dp_1'}, use_global_device_ids=true, to_apply=%add | all-reduce | flops 64 | bytes 512
  235.7 0.2 dynamic-update-slice.1
  235.9 0.2 dynamic-update-slice.5
  236.1 10.4 %all-reduce.9 = (f32[16]{0:T(128)S(1)}, f32[16]{0:T(128)S(1)}) all-reduce(f32[16]{0:T(128)S(1)} %dynamic-update-slice.1, f32[16]{0:T(128)S(1)} %dynamic-update-slice.5), channel_id=3, replica_groups=mesh['dp_0'=4,'dp_1'=8,'owner_0'=4,'owner_1'=2,'owner_2'=2] {'owner_0'}, use_global_device_ids=true, to_apply=%add.1 | all-reduce | flops 32 | bytes 256
  246.8 0.2 dynamic-update-slice.2
  247.9 9.8 %all-reduce.11 = (f32[8]{0:T(128)S(1)}, f32[8]{0:T(128)S(1)}) all-reduce(f32[8]{0:T(128)S(1)} %dynamic-update-slice.2, f32[8]{0:T(128)S(1)} %dynamic-update-slice.6), channel_id=4, replica_groups=mesh['dp_0'=4,'dp_1'=8,'owner_0'=4,'owner_1'=2,'owner_2'=2] {'owner_1'}, use_global_device_ids=true, to_apply=%add.2 | all-reduce | flops 16 | bytes 128
  257.9 0.2 dynamic-update-slice.3
  258.3 12.1 %all-reduce.10 = (f32[8]{0:T(128)S(1)}, f32[8]{0:T(128)S(1)}) all-reduce(f32[8]{0:T(128)S(1)} %dynamic-update-slice.3, f32[8]{0:T(128)S(1)} %dynamic-update-slice.7), channel_id=5, replica_groups=mesh['dp_0'=4,'dp_1'=8,'owner_0'=4,'owner_1'=2,'owner_2'=2] {'owner_2'}, use_global_device_ids=true, to_apply=%add.3 | all-reduce | flops 16 | bytes 128
  270.7 0.7 fusion.29
  272.8 0.6 fusion.26
  (41 shorter events, 1.8 us)
Async XLA Ops:
  0.0 1.0 copy-start
  3.5 68.7 %all-to-all-start = ((f32[32,32,512]{2,1,0:T(8,128)}), f32[32,32,512]{2,1,0:T(8,128)S(1)}, u32[]{:S(2)}, u32[]{:S(2)}) async-start(f32[32,32,512]{2,1,0:T(8,128)} %bitcast.40), calls=%async_computation | async-start | bytes 4194304 | tf_op jit(solution)/shard_map/all_to_all | solution.py:26
  72.3 5.0 %collective-permute-start = (f32[32,512]{1,0:T(8,128)S(1)}, f32[32,512]{1,0:T(8,128)S(1)}, u32[]{:S(2)}, u32[]{:S(2)}) collective-permute-start(f32[32,512]{1,0:T(8,128)S(1)} %reduce_sum.154), channel_id=1, source_target_pairs={{0,16},{16,0},{32,48},{48,32},{64,80},{80,64},{96,112},{112,96},{1... | collective-permute-start | bytes 196616 | tf_op jit(solution)/shard_map/ppermute | solution.py:15
  77.3 7.9 %collective-permute-start.1 = (f32[64,512]{1,0:T(8,128)S(1)}, f32[64,512]{1,0:T(8,128)S(1)}, u32[]{:S(2)}, u32[]{:S(2)}) collective-permute-start(f32[64,512]{1,0:T(8,128)S(1)} %maximum_select_fusion.3), channel_id=1, source_target_pairs={{0,32},{16,48},{32,0},{48,16},{64,96},{80,112},{96,64},{112,80},{1... | collective-permute-start | bytes 393224 | tf_op jit(solution)/shard_map/ppermute | solution.py:15
  85.2 14.8 %collective-permute-start.2 = (f32[128,512]{1,0:T(8,128)S(1)}, f32[128,512]{1,0:T(8,128)S(1)}, u32[]{:S(2)}, u32[]{:S(2)}) collective-permute-start(f32[128,512]{1,0:T(8,128)S(1)} %maximum_select_fusion.2), channel_id=1, source_target_pairs={{0,64},{16,80},{32,96},{48,112},{64,0},{80,16},{96,32},{112,48},{1... | collective-permute-start | bytes 786440 | tf_op jit(solution)/shard_map/ppermute | solution.py:15
  100.1 11.0 %collective-permute-start.3 = (f32[256,512]{1,0:T(8,128)S(1)}, f32[256,512]{1,0:T(8,128)S(1)}, u32[]{:S(2)}, u32[]{:S(2)}) collective-permute-start(f32[256,512]{1,0:T(8,128)S(1)} %maximum_select_fusion.1), channel_id=1, source_target_pairs={{0,128},{16,144},{32,160},{48,176},{64,192},{80,208},{96,224},{112... | collective-permute-start | bytes 1572872 | tf_op jit(solution)/shard_map/ppermute | solution.py:15
  111.1 7.9 %copy-start.1 = (f32[256,512]{1,0:T(8,128)}, f32[256,512]{1,0:T(8,128)S(1)}, u32[]{:S(2)}) copy-start(f32[256,512]{1,0:T(8,128)S(1)} %collective-permute-done.3) | copy-start | bytes 1572868
  171.4 37.9 %all-to-all-start.2 = ((f32[32,16,512]{2,1,0:T(8,128)}), f32[32,16,512]{2,1,0:T(8,128)S(1)}, u32[]{:S(2)}, u32[]{:S(2)}) async-start(f32[32,16,512]{2,1,0:T(8,128)} %fusion.48), calls=%async_computation.2 | async-start | bytes 2097152 | tf_op jit(solution)/shard_map/all_to_all | solution.py:26
